TPU v7x, 32 devices: a whole 2x2x4 slice. The times are simulated.
32 devices in a mesh: grp: 2 (over y), theta: 8 (over z, x), phi: 2 (over core).
Axes of the slice: x: 2, y: 2, z: 4, core: 2. Of those that a mesh axis runs over, the one named last changes fastest.
Arguments:
- maps: bfloat16 [8, 4096, 4096], P('grp', 'theta', 'phi'), parts along dimension 0, may hold values from -6 to 6
- deltas: bfloat16 [4096, 4, 4096], P('phi', None, 'theta'), may hold values from -1 to 1
- spin_rows: bfloat16 [4096, 2, 4], P('phi'), may hold values from -1 to 1
- ell_index: int32 [4], replicated, may hold values from 1024 to 2047
- owner_map: int32 [4096], replicated, may hold values from 0 to 4095, each once
- prior: float32 [4], replicated, may hold values from 0.3 to 3
Outputs:
- gradient: float32 [8, 2, 4096], P('grp', None, ('theta', 'phi')), parts along dimension 0
There are 2 independent parts, one for each index of `grp`. A program takes and returns all parts, laid end to end along the dimension named above; an argument that names none is the same for every part. Nothing has to cross between parts.
Inputs may be any that keep to these rules, and one draw needn't show every extreme that they name: `ell_index`: every selected degree is at least 1024; tables may repeat a degree. A permutation of the Fourier indices; slot s of deltas and of the output belongs to the frequency owner_map[s].
All inputs are finite; a program needn't handle non-finite values.
Results may differ from a plain program's by a relative error of at most 0.0003.
Values may be sent and summed in bfloat16 or wider, within the bound.
A program may use at most 256 MiB of HBM per device.

v0:
```python
import math
import jax
import jax.numpy as jnp
from jax import lax
from jax.sharding import PartitionSpec as P


def exact_einsum(form, table, operand):
    return jnp.einsum(form, table, operand, precision=lax.Precision.HIGHEST)


def angle_tables(row_count, start, count, modulus):
    freq_rows = jnp.arange(row_count, dtype=jnp.int32)
    sample_cols = start + jnp.arange(count, dtype=jnp.int32)
    angles = (
        2.0
        * math.pi
        / modulus
        * jnp.mod(freq_rows[:, None] * sample_cols[None, :], modulus).astype(jnp.float32)
    )
    return (jnp.cos(angles), jnp.sin(angles))


def row_transform(real_part, imag_part, outer_len, inner_len):
    row_count = real_part.shape[0]
    length = outer_len * inner_len
    cos_a, sin_a = angle_tables(outer_len, 0, outer_len, outer_len)
    real_blocks = real_part.reshape(row_count, outer_len, inner_len)
    section_real = exact_einsum("ka,rab->rkb", cos_a, real_blocks)
    section_imag = -exact_einsum("ka,rab->rkb", sin_a, real_blocks)
    if imag_part is not None:
        imag_blocks = imag_part.reshape(row_count, outer_len, inner_len)
        section_real = section_real + exact_einsum("ka,rab->rkb", sin_a, imag_blocks)
        section_imag = section_imag + exact_einsum("ka,rab->rkb", cos_a, imag_blocks)
    cos_t, sin_t = angle_tables(outer_len, 0, inner_len, length)
    turned_real = section_real * cos_t + section_imag * sin_t
    turned_imag = section_imag * cos_t - section_real * sin_t
    cos_b, sin_b = angle_tables(inner_len, 0, inner_len, inner_len)
    out_real = exact_einsum("qb,rkb->rqk", cos_b, turned_real) + exact_einsum(
        "qb,rkb->rqk", sin_b, turned_imag
    )
    out_imag = exact_einsum("qb,rkb->rqk", cos_b, turned_imag) - exact_einsum(
        "qb,rkb->rqk", sin_b, turned_real
    )
    return (out_real.reshape(row_count, length), out_imag.reshape(row_count, length))


def column_transform(real_part, imag_part, outer_len, inner_len, start):
    fields = real_part.shape[0]
    count = real_part.shape[2]
    slots = real_part.shape[3]
    length = outer_len * inner_len
    cos_a, sin_a = angle_tables(outer_len, 0, outer_len, outer_len)
    section_real = exact_einsum("ka,fabm->fkbm", cos_a, real_part) + exact_einsum(
        "ka,fabm->fkbm", sin_a, imag_part
    )
    section_imag = exact_einsum("ka,fabm->fkbm", cos_a, imag_part) - exact_einsum(
        "ka,fabm->fkbm", sin_a, real_part
    )
    cos_t, sin_t = angle_tables(outer_len, start, count, length)
    cos_t = cos_t[:, :, None]
    sin_t = sin_t[:, :, None]
    turned_real = section_real * cos_t + section_imag * sin_t
    turned_imag = section_imag * cos_t - section_real * sin_t
    cos_b, sin_b = angle_tables(inner_len, start, count, inner_len)
    out_real = exact_einsum("qb,fkbm->fqkm", cos_b, turned_real) + exact_einsum(
        "qb,fkbm->fqkm", sin_b, turned_imag
    )
    out_imag = exact_einsum("qb,fkbm->fqkm", cos_b, turned_imag) - exact_einsum(
        "qb,fkbm->fqkm", sin_b, turned_real
    )
    return (out_real.reshape(fields, length, slots), out_imag.reshape(fields, length, slots))


def accumulate(spectrum_block, table_block, spin_block, length, ell_index):
    count = table_block.shape[0]
    positions = jnp.arange(count, dtype=jnp.int32)
    freq = jnp.where(positions < length // 2, positions, positions - length)
    terms = []
    for degree in range(table_block.shape[1]):
        keep_rows = (jnp.abs(freq) <= ell_index[degree]).astype(jnp.float32)
        row_weights = spin_block[:, :, degree].astype(jnp.float32).T * keep_rows[None, :]
        table = table_block[:, degree, :].astype(jnp.float32)
        terms.append(
            jnp.einsum(
                "fk,ks,xfks->fxs",
                row_weights,
                table,
                spectrum_block,
                precision=lax.Precision.HIGHEST,
            )
        )
    return jnp.stack(terms)


def on_device(maps, deltas, spin_rows, ell_index, owner_map, prior):
    theta_count = lax.axis_size("theta")
    phi_count = lax.axis_size("phi")
    length = maps.shape[2] * phi_count
    values = maps.astype(jnp.float32)
    planes = jnp.stack([values[0], values[1] * values[2], values[1] * values[3]])
    row_planes = lax.all_to_all(planes, "phi", split_axis=1, concat_axis=2, tiled=True)
    inner_len = length // theta_count
    spectra = [
        row_transform(row_planes[0], None, theta_count, inner_len),
        row_transform(row_planes[1], row_planes[2], theta_count, inner_len),
    ]
    stacked = jnp.stack(
        [
            jnp.stack([spectrum[0] for spectrum in spectra]),
            jnp.stack([spectrum[1] for spectrum in spectra]),
        ]
    )
    permuted = jnp.take(stacked, owner_map, axis=3)
    columns = lax.all_to_all(permuted, "theta", split_axis=3, concat_axis=2, tiled=True)
    fields = columns.shape[1]
    slots = columns.shape[3]
    sub_rows = columns.shape[2] // theta_count
    blocks = columns.reshape(2, fields, theta_count, sub_rows, slots)
    row_start = lax.axis_index("phi") * sub_rows
    spec_real, spec_imag = column_transform(blocks[0], blocks[1], theta_count, inner_len, row_start)
    combined = jnp.stack([spec_real, spec_imag])
    totals = accumulate(
        combined,
        lax.all_gather(deltas, "phi", axis=0, tiled=True),
        lax.all_gather(spin_rows, "phi", axis=0, tiled=True),
        length,
        ell_index,
    )
    shares = lax.psum_scatter(totals, "phi", scatter_dimension=3, tiled=True)
    share_count = shares.shape[3]
    slot_start = lax.axis_index("theta") * slots + lax.axis_index("phi") * share_count
    share_ids = lax.dynamic_slice_in_dim(owner_map, slot_start, share_count)
    slot_freq = jnp.where(share_ids < length // 2, share_ids, share_ids - length)
    ell_float = ell_index.astype(jnp.float32)
    weight = 2.0 * math.pi / length * jnp.sqrt((2.0 * ell_float + 1.0) / (4.0 * math.pi)) / length
    keep_slots = (jnp.abs(slot_freq)[None, :] <= ell_index[:, None]).astype(jnp.float32) * weight[
        :, None
    ]
    scalar_real = shares[:, 0, 0] * keep_slots
    scalar_imag = shares[:, 0, 1] * keep_slots
    spin_real = shares[:, 1, 0] * keep_slots
    spin_imag = shares[:, 1, 1] * keep_slots
    coupling = (prior * jnp.sqrt(ell_float * (ell_float + 1.0)) / (length // 2))[:, None]
    inner_real = -spin_imag - coupling * scalar_real
    inner_imag = spin_real - coupling * scalar_imag
    turns = jnp.mod(-slot_freq, 4)
    phase_real = jnp.where(turns == 0, 1.0, jnp.where(turns == 2, -1.0, 0.0)).astype(jnp.float32)[
        None, :
    ]
    phase_imag = jnp.where(turns == 1, 1.0, jnp.where(turns == 3, -1.0, 0.0)).astype(jnp.float32)[
        None, :
    ]
    out_real = phase_real * inner_real - phase_imag * inner_imag
    out_imag = phase_real * inner_imag + phase_imag * inner_real
    return jnp.stack([out_real, out_imag], axis=1)


def solution(mesh):
    placed = (
        P("grp", "theta", "phi"),
        P("phi", None, "theta"),
        P("phi", None, None),
        P(),
        P(),
        P(),
    )
    return jax.shard_map(
        on_device,
        mesh=mesh,
        in_specs=placed,
        out_specs=P("grp", None, ("theta", "phi")),
        check_vma=False,
    )
```

profile of v0, /device:TPU:0, one launch (start us, length us, event | category | flops | bytes accessed | tf_op | source)
XLA Modules:
  0.0 1105.6 jit_solution(13020259938788177995)
XLA Ops:
  6.5 11.3 %convert_element_type.145 = f32[4,512,2048]{2,1,0:T(8,128)} convert(bf16[4,512,2048]{2,1,0:T(8,128)(2,1)} %param.6) | non-fusion elementwise | flops 4194304 | bytes 25165824 | tf_op jit(solution)/shard_map/convert_element_type | solution.py:100
  40.1 16.7 %copy.115 = f32[3,512,2048]{2,0,1:T(4,128)S(1)} copy(f32[3,512,2048]{2,1,0:T(8,128)} %pad_maximum_fusion.1) | data formatting | bytes 25165824 | tf_op jit(solution)/shard_map/stack | solution.py:101
  56.8 17.4 %all_to_all.30 = f32[3,512,2048]{2,0,1:T(4,128)S(1)} all-to-all(f32[3,512,2048]{2,0,1:T(4,128)S(1)} %copy.115), channel_id=1, replica_groups=mesh['grp'=2,'theta'=8,'phi'=2] {'phi'}, dimensions={1} | all-to-all | bytes 25165824 | tf_op jit(solution)/shard_map/all_to_all | solution.py:102
  74.2 14.4 %copy.241 = f32[3,2,256,2048]{3,1,2,0:T(2,128)} copy(f32[3,2,256,2048]{3,0,2,1:T(4,128)S(1)} %bitcast.262) | data formatting | bytes 25165824 | tf_op jit(solution)/shard_map/all_to_all | solution.py:102
  155.5 10.5 fusion.24
  166.0 13.1 %fusion.36 = f32[256,8,512]{2,0,1:T(8,128)S(1)} fusion(f32[256,8,512]{2,1,0:T(8,128)S(1)} %get-tuple-element.26), kind=kOutput, calls=%fused_computation.77 | convolution fusion | flops 6446120960 | bytes 8388608 | tf_op jit(solution)/shard_map/qb,rkb->rqk/dot_general | solution.py:9
  179.0 15.6 %fusion.34 = f32[256,8,512]{2,0,1:T(8,128)} fusion(f32[256,8,512]{2,1,0:T(8,128)S(1)} %get-tuple-element.26), kind=kOutput, calls=%fused_computation.75 | convolution fusion | flops 6446120960 | bytes 8388608 | tf_op jit(solution)/shard_map/qb,rkb->rqk/dot_general | solution.py:9
  194.6 15.8 %fusion.28 = f32[256,8,512]{2,0,1:T(8,128)} fusion(f32[256,8,512]{2,1,0:T(8,128)S(1)} %get-tuple-element.37), kind=kOutput, calls=%fused_computation.69 | convolution fusion | flops 6446120960 | bytes 8388608 | tf_op jit(solution)/shard_map/qb,rkb->rqk/dot_general | solution.py:9
  210.4 16.0 %fusion.26 = f32[256,8,512]{2,0,1:T(8,128)} fusion(f32[256,8,512]{2,1,0:T(8,128)S(1)} %get-tuple-element.37), kind=kOutput, calls=%fused_computation.67 | convolution fusion | flops 6446120960 | bytes 8388608 | tf_op jit(solution)/shard_map/qb,rkb->rqk/dot_general | solution.py:9
  226.5 15.9 %add_bitcast_fusion.2 = f32[256,512,8]{1,0,2:T(8,128)} fusion(f32[256,8,512]{2,0,1:T(8,128)S(1)} %fusion.36, f32[256,8,512]{2,1,0:T(8,128)S(1)} %get-tuple-element.25), kind=kOutput, calls=%fused_computation.66 | convolution fusion | flops 6447169536 | bytes 12582912 | tf_op jit(solution)/shard_map/qb,rkb->rqk/dot_general | solution.py:9
  257.3 15.8 %add_bitcast_fusion.1 = f32[256,512,8]{1,0,2:T(8,128)} fusion(f32[256,8,512]{2,0,1:T(8,128)S(1)} %copy-done.13, f32[256,8,512]{2,1,0:T(8,128)S(1)} %copy-done.4), kind=kOutput, calls=%fused_computation.64 | convolution fusion | flops 6447169536 | bytes 12582912 | tf_op jit(solution)/shard_map/qb,rkb->rqk/dot_general | solution.py:9
  288.1 16.1 %subtract_bitcast_fusion.2 = f32[256,512,8]{1,0,2:T(8,128)} fusion(f32[256,8,512]{2,0,1:T(8,128)S(1)} %copy-done.12, f32[256,8,512]{2,1,0:T(8,128)S(1)} %copy-done.7), kind=kOutput, calls=%fused_computation.63 | convolution fusion | flops 6447169536 | bytes 12582912 | tf_op jit(solution)/shard_map/qb,rkb->rqk/dot_general | solution.py:9
  319.1 15.8 %subtract_bitcast_fusion.1 = f32[256,512,8]{1,0,2:T(8,128)} fusion(f32[256,8,512]{2,0,1:T(8,128)S(1)} %copy-done.11, f32[256,8,512]{2,1,0:T(8,128)S(1)} %copy-done.5), kind=kOutput, calls=%fused_computation.62 | convolution fusion | flops 6447169536 | bytes 12582912 | tf_op jit(solution)/shard_map/qb,rkb->rqk/dot_general | solution.py:9
  372.4 52.5 %gather_fusion = f32[4096,2,2,256]{3,2,1,0:T(2,128)} fusion(f32[2,2,256,4096]{2,1,3,0:T(2,128)} %pad_maximum_fusion, s32[4096]{0:T(1024)S(1)} %fusion.105), kind=kCustom, calls=%fused_computation | custom fusion | bytes 33570816 | tf_op jit(solution)/shard_map/jit(_take)/gather | solution.py:114
  424.9 17.6 %select_bitcast_fusion = f32[2,2,256,4096]{2,1,0,3:T(2,128)} fusion(f32[4096,2,2,256]{3,2,1,0:T(2,128)} %gather_fusion, pred[4096]{0:T(1024)(128)(4,1)S(1)} %compare_and_fusion), kind=kLoop, calls=%fused_computation.9 | loop fusion | flops 4194304 | bytes 33558528 | tf_op jit(solution)/shard_map/jit(_take)/select_n | solution.py:114
  472.9 17.0 %all-gather.2.cloned.1.call-done = bf16[4096,4,512]{2,0,1:T(8,128)(2,1)} async-done(((bf16[2048,4,512]{2,0,1:T(8,128)(2,1)}), bf16[4096,4,512]{2,0,1:T(8,128)(2,1)}) %all-gather.2.cloned.1.call-update) | async-done | bytes 16777232 | tf_op jit(solution)/shard_map/all_gather | solution.py:125
  489.9 15.4 %fusion.18 = (f32[4096,512]{1,0:T(8,128)}, f32[4096,512]{1,0:T(8,128)}, f32[4096,512]{1,0:T(8,128)}, f32[4096,512]{1,0:T(8,128)}) fusion(bf16[4096,4,512]{2,0,1:T(8,128)(2,1)} %all-gather.2.cloned.1.call-done), kind=kLoop, calls=%fused_computation.41 | loop fusion | flops 8388608 | bytes 50331648 | tf_op jit(solution)/shard_map/convert.15
  505.3 20.2 %multiply_bitcast_fusion = (f32[2,512,4096]{1,0,2:T(2,128)}, f32[2,512,4096]{1,0,2:T(2,128)}) fusion(f32[4096,512]{1,0:T(8,128)} %get-tuple-element.16, f32[4096,2]{1,0:T(8,128)} %copy.144, f32[4096,512]{1,0:T(8,128)} %get-tuple-element.17, f32[4096,2]{1,0:T(8,128)S(1)} %copy.143), kind=kLoop, calls=%fused_computation.10 | loop fusion | flops 8388608 | bytes 50397184
  525.4 15.2 %copy.190 = f32[2,512,4096]{1,2,0:T(8,128)} copy(f32[2,512,4096]{1,0,2:T(2,128)} %get-tuple-element.48) | data formatting | bytes 33554432
  550.8 20.1 %multiply_bitcast_fusion.2 = (f32[2,512,4096]{1,0,2:T(2,128)}, f32[2,512,4096]{1,0,2:T(2,128)}) fusion(f32[4096,512]{1,0:T(8,128)} %get-tuple-element.18, f32[4096,2]{1,0:T(8,128)} %copy.142, f32[4096,512]{1,0:T(8,128)} %get-tuple-element.19, f32[4096,2]{1,0:T(8,128)S(1)} %copy-done.18), kind=kLoop, calls=%fused_computation.12 | loop fusion | flops 8388608 | bytes 50397184
  571.0 15.2 %copy.188 = f32[2,512,4096]{1,2,0:T(8,128)} copy(f32[2,512,4096]{1,0,2:T(2,128)} %get-tuple-element.50) | data formatting | bytes 33554432
  596.3 216.9 %all-to-all-done.1 = f32[2,2,256,4096]{2,1,0,3:T(2,128)} async-done(((f32[2,2,256,4096]{2,1,0,3:T(2,128)}), f32[2,2,256,4096]{2,1,0,3:T(2,128)}, u32[]{:S(2)}, u32[]{:S(2)}) %all-to-all-start.1) | async-done | bytes 16777248 | tf_op jit(solution)/shard_map/all_to_all | solution.py:115
  813.2 19.4 %copy.177 = f32[2,2,256,8,512]{4,3,2,1,0:T(8,128)} copy(f32[2,2,256,8,512]{2,1,0,4,3:T(2,128)} %bitcast.33) | data formatting | bytes 33554432 | tf_op jit(solution)/shard_map/all_to_all | solution.py:115
  832.6 11.8 %fusion.2 = f32[2,256,512,8]{2,3,1,0:T(8,128)} fusion(f32[2,2,8,256,512]{4,2,3,1,0:T(8,128)} %bitcast.258), kind=kOutput, calls=%fused_computation.28 | convolution fusion | flops 201327488 | bytes 16777216 | tf_op jit(solution)/shard_map/ka,fabm->fkbm/dot_general | solution.py:9
  863.2 21.9 %fusion = (f32[2,8,256,512]{3,1,2,0:T(8,128)}, f32[2,8,256,512]{3,1,2,0:T(8,128)}) fusion(f32[8,256]{0,1:T(8,128)S(1)} %copy.135, f32[8,256]{0,1:T(8,128)S(1)} %copy.134, f32[2,256,512,8]{2,3,1,0:T(8,128)} %fusion.2, f32[2,256,512,8]{2,3,1,0:T(8,128)} %fusion.3, f32[2,256,512,8]{2,3,1,0:T(8,128)} %fusion.5, f32[2,2,8,256,512]{4,2,3,1,0:T(8,128)} %bitcast.259), kind=kOutput, calls=%fused_computation.24 | convolution fusion | flops 218104704 | bytes 50348032 | tf_op jit(solution)/shard_map/ka,fabm->fkbm/dot_general | solution.py:9
  885.1 26.0 %fusion.8 = f32[2,8,512,512]{2,3,1,0:T(8,128)} fusion(f32[2,8,256,512]{3,1,2,0:T(8,128)} %get-tuple-element.15, s32[256]{0:T(256)S(1)} %iota_add_fusion), kind=kOutput, calls=%fused_computation.34 | convolution fusion | flops 12886736896 | bytes 25166848 | tf_op jit(solution)/shard_map/qb,fkbm->fqkm/dot_general | solution.py:9
  911.1 25.8 %fusion.6 = f32[2,8,512,512]{2,3,1,0:T(8,128)S(1)} fusion(f32[2,8,256,512]{3,1,2,0:T(8,128)} %get-tuple-element.15, s32[256]{0:T(256)S(1)} %iota_add_fusion), kind=kOutput, calls=%fused_computation.32 | convolution fusion | flops 12886736896 | bytes 25166848 | tf_op jit(solution)/shard_map/qb,fkbm->fqkm/dot_general | solution.py:9
  936.9 49.7 %add_bitcast_fusion = f32[2,512,8,512]{3,1,2,0:T(8,128)} fusion(f32[2,8,512,512]{2,3,1,0:T(8,128)} %fusion.8, f32[2,8,256,512]{3,1,2,0:T(8,128)} %get-tuple-element.14, s32[256]{0:T(256)S(1)} %iota_add_fusion), kind=kOutput, calls=%fused_computation.14 | convolution fusion | flops 12890931200 | bytes 41944064 | tf_op jit(solution)/shard_map/qb,fkbm->fqkm/dot_general | solution.py:9
  986.6 17.7 %copy.240 = f32[2,512,8,512]{3,2,1,0:T(8,128)} copy(f32[2,512,8,512]{3,1,2,0:T(8,128)} %add_bitcast_fusion) | data formatting | bytes 33554432 | tf_op jit(solution)/shard_map/add | solution.py:66
  1004.4 27.7 %subtract_bitcast_fusion = f32[2,512,8,512]{3,1,2,0:T(8,128)} fusion(f32[2,8,512,512]{2,3,1,0:T(8,128)S(1)} %fusion.6, f32[2,8,256,512]{3,1,2,0:T(8,128)} %get-tuple-element.14, s32[256]{0:T(256)S(1)} %iota_add_fusion), kind=kOutput, calls=%fused_computation.13 | convolution fusion | flops 12890931200 | bytes 41944064 | tf_op jit(solution)/shard_map/qb,fkbm->fqkm/dot_general | solution.py:9
  1032.1 19.3 %copy.239 = f32[2,512,8,512]{3,2,1,0:T(8,128)} copy(f32[2,512,8,512]{3,1,2,0:T(8,128)} %subtract_bitcast_fusion) | data formatting | bytes 33554432 | tf_op jit(solution)/shard_map/sub | solution.py:69
  1051.5 27.6 %multiply_reduce_fusion.3 = (f32[2,512,2]{1,0,2:T(2,128)S(1)}, f32[2,512,2]{1,0,2:T(2,128)S(1)}, f32[2,512,2]{1,0,2:T(2,128)S(1)}, f32[2,512,2]{1,0,2:T(2,128)S(1)}) fusion(f32[2,512,4096]{1,2,0:T(8,128)} %copy.188, f32[1,2,4096,512]{3,2,1,0:T(8,128)} %bitcast.264, f32[1,2,4096,512]{3,2,1,0:T(8,128)S(1)} %bitcast.263, f32[2,512,4096]{1,2,0:T(8,128)} %copy.189, ...), kind=kLoop, calls=%fused_computation.5 | loop fusion | flops 75489280 | bytes 100696064 | tf_op jit(solution)/shard_map/fk,ks,xfks->fxs/dot_general | solution.py:85
  (128 shorter events, 260.1 us)
Async XLA Ops:
  104.0 8.7 copy-start.10
  124.7 10.2 copy-start.8
  124.7 10.2 copy-start.14
  146.8 8.6 copy-start.9
  165.9 60.5 %copy-start.6 = (f32[256,8,512]{2,1,0:T(8,128)}, f32[256,8,512]{2,1,0:T(8,128)S(1)}, u32[]{:S(2)}) copy-start(f32[256,8,512]{2,1,0:T(8,128)S(1)} %get-tuple-element.25) | copy-start | bytes 12582916
  194.6 31.8 %copy-start.19 = (s32[4096]{0:T(1024)S(1)}, s32[4096]{0:T(1024)}, u32[]{:S(2)}) copy-start(s32[4096]{0:T(1024)} %param.10) | copy-start | bytes 49156
  247.8 9.5 copy-start.4
  247.8 9.5 copy-start.13
  278.6 9.5 copy-start.7
  278.6 9.5 copy-start.12
  309.6 9.5 copy-start.5
  309.6 9.5 copy-start.11
  340.4 7.9 copy-start.15
  340.4 7.9 copy-start.16
  348.3 7.7 copy-start.17
  442.5 370.7 %all-to-all-start.1 = ((f32[2,2,256,4096]{2,1,0,3:T(2,128)}), f32[2,2,256,4096]{2,1,0,3:T(2,128)}, u32[]{:S(2)}, u32[]{:S(2)}) async-start(f32[2,2,256,4096]{2,1,0,3:T(2,128)} %select_bitcast_fusion), calls=%async_computation.1 | async-start | bytes 33554432 | tf_op jit(solution)/shard_map/all_to_all | solution.py:115
  449.8 40.1 %all-gather.2.cloned.1.call-start = ((), (), s32[]{:S(2)}) async-start(), calls=%async_computation.3 | async-start | bytes 25165824 | tf_op jit(solution)/shard_map/all_gather | solution.py:125
  458.2 0.8 copy-start.20
  458.2 2.6 copy-start.21
  458.2 14.1 %copy-start.27 = (f32[4]{0:T(128)S(1)}, f32[4]{0:T(128)}, u32[]{:S(2)}) copy-start(f32[4]{0:T(128)} %param.11) | copy-start | bytes 52
  458.3 632.6 %reduce-scatter.4.cloned.1.call-start = ((), (), s32[]{:S(2)}) async-start(), calls=%async_computation.4 | async-start | bytes 393216
  525.4 16.5 %copy-start.1 = (f32[2,512,4096]{1,0,2:T(2,128)S(1)}, f32[2,512,4096]{1,0,2:T(2,128)}, u32[]{:S(2)}) copy-start(f32[2,512,4096]{1,0,2:T(2,128)} %get-tuple-element.47) | copy-start | bytes 50331652
  541.9 8.9 copy-start.18
  570.9 16.5 %copy-start.2 = (f32[2,512,4096]{1,0,2:T(2,128)S(1)}, f32[2,512,4096]{1,0,2:T(2,128)}, u32[]{:S(2)}) copy-start(f32[2,512,4096]{1,0,2:T(2,128)} %get-tuple-element.49) | copy-start | bytes 50331652
  832.6 11.8 %copy-start = (f32[2,2,256,8,512]{4,3,2,1,0:T(8,128)S(1)}, f32[2,2,256,8,512]{4,3,2,1,0:T(8,128)}, u32[]{:S(2)}) copy-start(f32[2,2,256,8,512]{4,3,2,1,0:T(8,128)} %copy.177) | copy-start | bytes 50331652
  1032.1 19.4 %copy-start.3 = (f32[2,512,8,512]{3,2,1,0:T(8,128)S(1)}, f32[2,512,8,512]{3,2,1,0:T(8,128)}, u32[]{:S(2)}) copy-start(f32[2,512,8,512]{3,2,1,0:T(8,128)} %copy.240) | copy-start | bytes 50331652
  1079.1 18.7 %copy-start.22 = (s32[4]{0:T(128)S(1)}, s32[4]{0:T(128)}, u32[]{:S(2)}) copy-start(s32[4]{0:T(128)} %param.9) | copy-start | bytes 52
  1079.1 18.7 %copy-start.23 = (f32[256]{0:T(256)S(1)}, f32[256]{0:T(256)}, u32[]{:S(2)}) copy-start(f32[256]{0:T(256)} %get-tuple-element.12) | copy-start | bytes 3076
  1079.1 18.7 %copy-start.24 = (f32[256]{0:T(256)S(1)}, f32[256]{0:T(256)}, u32[]{:S(2)}) copy-start(f32[256]{0:T(256)} %compare_select_fusion.7) | copy-start | bytes 3076
  1079.1 18.7 %copy-start.25 = (f32[4]{0:T(128)S(1)}, f32[4]{0:T(128)}, u32[]{:S(2)}) copy-start(f32[4]{0:T(128)} %get-tuple-element.41) | copy-start | bytes 52
  1079.1 18.7 %copy-start.26 = (f32[4]{0:T(128)S(1)}, f32[4]{0:T(128)}, u32[]{:S(2)}) copy-start(f32[4]{0:T(128)} %get-tuple-element.42) | copy-start | bytes 52
Sparse Core Ops, SparseCore 0:
  458.4 31.4 all-gather.1
  1084.0 6.7 reduce-scatter.3
where the time goes:
time: 1110 us
  matrix products  354 us (32%)
  local copies, waits for them, and re-layouts  310 us (28%)
  waiting for transfers between devices  240 us (22%)
  other arithmetic  161 us (15%)
  blocking collectives  19.2 us (2%)
  between operations  14.1 us (1%)
    dot_general x22, matrix products, exact_einsum(): return jnp.einsum(form, table, operand, precision=lax.Precision.HIGHEST)  354 us
    all_to_all x1, waiting for transfers between devices, on_device(): lax.all_to_all(permuted, 'theta', split_axis=3, concat_axis=2, tiled=True)  217 us
    unnamed x68, local copies, waits for them, and re-layouts  68.2 us
    gather x1, local copies, waits for them, and re-layouts, on_device(): permuted = jnp.take(stacked, owner_map, axis=3)  52.5 us
    unnamed x2, other arithmetic  40.3 us
    dot_general x1, other arithmetic, accumulate(): jnp.einsum('fk,ks,xfks->fxs', row_weights, table, spectrum_block, precisi...  27.6 us
    another operation x3, other arithmetic, on_device(): jnp.stack([jnp.stack([spectrum[0] for spectrum in spectra]), jnp.stack([s...  24 us
  transfers between devices with their start and end apart: 3, of which 3 were waited for; matrix products, arithmetic and copies ran while one was open for 11% of the time, Pallas kernels for 0%

commit v1 on v0

--- a/solution.py
+++ b/solution.py
@@ -112,7 +112,12 @@
         ]
     )
     permuted = jnp.take(stacked, owner_map, axis=3)
-    columns = lax.all_to_all(permuted, "theta", split_axis=3, concat_axis=2, tiled=True)
+    columns = jnp.concatenate(
+        lax.all_to_all(
+            jnp.stack(jnp.split(permuted, lax.axis_size("theta"), axis=3)), "theta", 0, 0
+        ),
+        axis=2,
+    )
     fields = columns.shape[1]
     slots = columns.shape[3]
     sub_rows = columns.shape[2] // theta_count

time: 1110 us -> 1150 us (1.036)
  local copies, waits for them, and re-layouts: 310 us -> 347 us
    another operation x0 -> x2, local copies, waits for them, and re-layouts: none -> 27.1 us  [on_device(): jnp.stack(jnp.split(permuted, lax.axis_size('theta'), axis=3))]
    unnamed x68 -> x75, local copies, waits for them, and re-layouts: 68.2 us -> 82.8 us
where the time goes in v1:
time: 1150 us; the launch traced here: 1140 us
  matrix products  352 us (31%)
  local copies, waits for them, and re-layouts  347 us (30%)
  waiting for transfers between devices  240 us (21%)
  other arithmetic  160 us (14%)
  blocking collectives  19.2 us (2%)
  between operations  14.1 us (1%)
    dot_general x22, matrix products, exact_einsum(): return jnp.einsum(form, table, operand, precision=lax.Precision.HIGHEST)  352 us
    all_to_all x1, waiting for transfers between devices, on_device(): lax.all_to_all(jnp.stack(jnp.split(permuted, lax.axis_size('theta'), axis...  217 us
    unnamed x75, local copies, waits for them, and re-layouts  82.8 us
    gather x1, local copies, waits for them, and re-layouts, on_device(): permuted = jnp.take(stacked, owner_map, axis=3)  52.4 us
    unnamed x2, other arithmetic  40.3 us
    dot_general x1, other arithmetic, accumulate(): jnp.einsum('fk,ks,xfks->fxs', row_weights, table, spectrum_block, precisi...  27.6 us
    another operation x2, local copies, waits for them, and re-layouts, on_device(): jnp.stack(jnp.split(permuted, lax.axis_size('theta'), axis=3))  27.1 us
    another operation x3, other arithmetic, on_device(): jnp.stack([jnp.stack([spectrum[0] for spectrum in spectra]), jnp.stack([s...  24.1 us
  transfers between devices with their start and end apart: 3, of which 3 were waited for; matrix products, arithmetic and copies ran while one was open for 11% of the time, Pallas kernels for 0%

profile of v1, /device:TPU:0, one launch (start us, length us, event | category | flops | bytes accessed | tf_op | source)
XLA Modules:
  0.0 1139.7 jit_solution(17851256556611671881)
XLA Ops:
  6.5 11.3 convert_element_type.145
  40.1 16.7 %copy.131 = f32[3,512,2048]{2,0,1:T(4,128)S(1)} copy(f32[3,512,2048]{2,1,0:T(8,128)} %pad_maximum_fusion.1) | data formatting | bytes 25165824 | tf_op jit(solution)/shard_map/stack | solution.py:101
  56.8 17.4 %all_to_all.20 = f32[3,512,2048]{2,0,1:T(4,128)S(1)} all-to-all(f32[3,512,2048]{2,0,1:T(4,128)S(1)} %copy.131), channel_id=1, replica_groups=mesh['grp'=2,'theta'=8,'phi'=2] {'phi'}, dimensions={1} | all-to-all | bytes 25165824 | tf_op jit(solution)/shard_map/all_to_all | solution.py:102
  74.2 14.4 %copy.259 = f32[3,2,256,2048]{3,1,2,0:T(2,128)} copy(f32[3,2,256,2048]{3,0,2,1:T(4,128)S(1)} %bitcast.295) | data formatting | bytes 25165824 | tf_op jit(solution)/shard_map/all_to_all | solution.py:102
  155.5 10.5 fusion.24
  166.0 13.1 %fusion.36 = f32[256,8,512]{2,0,1:T(8,128)S(1)} fusion(f32[256,8,512]{2,1,0:T(8,128)S(1)} %get-tuple-element.26), kind=kOutput, calls=%fused_computation.78 | convolution fusion | flops 6446120960 | bytes 8388608 | tf_op jit(solution)/shard_map/qb,rkb->rqk/dot_general | solution.py:9
  179.0 15.6 %fusion.34 = f32[256,8,512]{2,0,1:T(8,128)} fusion(f32[256,8,512]{2,1,0:T(8,128)S(1)} %get-tuple-element.26), kind=kOutput, calls=%fused_computation.76 | convolution fusion | flops 6446120960 | bytes 8388608 | tf_op jit(solution)/shard_map/qb,rkb->rqk/dot_general | solution.py:9
  194.6 15.8 %fusion.28 = f32[256,8,512]{2,0,1:T(8,128)} fusion(f32[256,8,512]{2,1,0:T(8,128)S(1)} %get-tuple-element.37), kind=kOutput, calls=%fused_computation.70 | convolution fusion | flops 6446120960 | bytes 8388608 | tf_op jit(solution)/shard_map/qb,rkb->rqk/dot_general | solution.py:9
  210.4 16.0 %fusion.26 = f32[256,8,512]{2,0,1:T(8,128)} fusion(f32[256,8,512]{2,1,0:T(8,128)S(1)} %get-tuple-element.37), kind=kOutput, calls=%fused_computation.68 | convolution fusion | flops 6446120960 | bytes 8388608 | tf_op jit(solution)/shard_map/qb,rkb->rqk/dot_general | solution.py:9
  226.5 15.9 %add_bitcast_fusion.2 = f32[256,512,8]{1,0,2:T(8,128)} fusion(f32[256,8,512]{2,0,1:T(8,128)S(1)} %fusion.36, f32[256,8,512]{2,1,0:T(8,128)S(1)} %get-tuple-element.25), kind=kOutput, calls=%fused_computation.67 | convolution fusion | flops 6447169536 | bytes 12582912 | tf_op jit(solution)/shard_map/qb,rkb->rqk/dot_general | solution.py:9
  257.3 15.8 %add_bitcast_fusion.1 = f32[256,512,8]{1,0,2:T(8,128)} fusion(f32[256,8,512]{2,0,1:T(8,128)S(1)} %copy-done.13, f32[256,8,512]{2,1,0:T(8,128)S(1)} %copy-done.4), kind=kOutput, calls=%fused_computation.65 | convolution fusion | flops 6447169536 | bytes 12582912 | tf_op jit(solution)/shard_map/qb,rkb->rqk/dot_general | solution.py:9
  288.1 16.1 %subtract_bitcast_fusion.2 = f32[256,512,8]{1,0,2:T(8,128)} fusion(f32[256,8,512]{2,0,1:T(8,128)S(1)} %copy-done.12, f32[256,8,512]{2,1,0:T(8,128)S(1)} %copy-done.7), kind=kOutput, calls=%fused_computation.64 | convolution fusion | flops 6447169536 | bytes 12582912 | tf_op jit(solution)/shard_map/qb,rkb->rqk/dot_general | solution.py:9
  319.1 15.8 %subtract_bitcast_fusion.1 = f32[256,512,8]{1,0,2:T(8,128)} fusion(f32[256,8,512]{2,0,1:T(8,128)S(1)} %copy-done.11, f32[256,8,512]{2,1,0:T(8,128)S(1)} %copy-done.5), kind=kOutput, calls=%fused_computation.63 | convolution fusion | flops 6447169536 | bytes 12582912 | tf_op jit(solution)/shard_map/qb,rkb->rqk/dot_general | solution.py:9
  372.4 52.4 %gather_fusion = f32[4096,2,2,256]{3,2,1,0:T(2,128)} fusion(f32[2,2,256,4096]{2,1,3,0:T(2,128)} %pad_maximum_fusion, s32[4096]{0:T(1024)S(1)} %fusion.113), kind=kCustom, calls=%fused_computation | custom fusion | bytes 33570816 | tf_op jit(solution)/shard_map/jit(_take)/gather | solution.py:114
  424.8 16.4 %select_bitcast_fusion = f32[2,2,256,4096]{2,1,0,3:T(2,128)S(1)} fusion(f32[4096,2,2,256]{3,2,1,0:T(2,128)} %gather_fusion, pred[4096]{0:T(1024)(128)(4,1)S(1)} %compare_and_fusion), kind=kLoop, calls=%fused_computation.10 | loop fusion | flops 4194304 | bytes 33558528 | tf_op jit(solution)/shard_map/jit(_take)/select_n | solution.py:114
  457.9 25.0 %copy.149 = f32[8,2,2,256,512]{4,3,2,1,0:T(8,128)} copy(f32[8,2,2,256,512]{3,2,1,4,0:T(2,128)} %fusion.50) | data formatting | bytes 33554432 | tf_op jit(solution)/shard_map/stack | solution.py:117
  513.3 17.0 %all-gather.2.cloned.1.call-done = bf16[4096,4,512]{2,0,1:T(8,128)(2,1)} async-done(((bf16[2048,4,512]{2,0,1:T(8,128)(2,1)}), bf16[4096,4,512]{2,0,1:T(8,128)(2,1)}) %all-gather.2.cloned.1.call-update) | async-done | bytes 16777232 | tf_op jit(solution)/shard_map/all_gather | solution.py:130
  530.3 15.8 %fusion.18 = (f32[4096,512]{1,0:T(8,128)}, f32[4096,512]{1,0:T(8,128)}, f32[4096,512]{1,0:T(8,128)}, f32[4096,512]{1,0:T(8,128)}) fusion(bf16[4096,4,512]{2,0,1:T(8,128)(2,1)} %all-gather.2.cloned.1.call-done), kind=kLoop, calls=%fused_computation.42 | loop fusion | flops 8388608 | bytes 50331648 | tf_op jit(solution)/shard_map/convert.15
  546.0 20.2 %multiply_bitcast_fusion = (f32[2,512,4096]{1,0,2:T(2,128)}, f32[2,512,4096]{1,0,2:T(2,128)}) fusion(f32[4096,512]{1,0:T(8,128)} %get-tuple-element.16, f32[4096,2]{1,0:T(8,128)} %copy.161, f32[4096,512]{1,0:T(8,128)} %get-tuple-element.17, f32[4096,2]{1,0:T(8,128)S(1)} %copy.160), kind=kLoop, calls=%fused_computation.11 | loop fusion | flops 8388608 | bytes 50397184
  566.2 15.2 %copy.206 = f32[2,512,4096]{1,2,0:T(8,128)} copy(f32[2,512,4096]{1,0,2:T(2,128)} %get-tuple-element.48) | data formatting | bytes 33554432
  591.6 20.1 %multiply_bitcast_fusion.2 = (f32[2,512,4096]{1,0,2:T(2,128)}, f32[2,512,4096]{1,0,2:T(2,128)}) fusion(f32[4096,512]{1,0:T(8,128)} %get-tuple-element.18, f32[4096,2]{1,0:T(8,128)} %copy.159, f32[4096,512]{1,0:T(8,128)} %get-tuple-element.19, f32[4096,2]{1,0:T(8,128)S(1)} %copy-done.18), kind=kLoop, calls=%fused_computation.13 | loop fusion | flops 8388608 | bytes 50397184
  611.7 15.2 %copy.204 = f32[2,512,4096]{1,2,0:T(8,128)} copy(f32[2,512,4096]{1,0,2:T(2,128)} %get-tuple-element.50) | data formatting | bytes 33554432
  637.1 216.5 %all-to-all-done.1 = f32[8,2,2,256,512]{4,3,2,1,0:T(8,128)} async-done(((f32[8,2,2,256,512]{4,3,2,1,0:T(8,128)}), f32[8,2,2,256,512]{4,3,2,1,0:T(8,128)}, u32[]{:S(2)}, u32[]{:S(2)}) %all-to-all-start.1) | async-done | bytes 16777248 | tf_op jit(solution)/shard_map/all_to_all | solution.py:116
  853.6 15.4 %copy.258 = f32[8,2,2,256,512]{4,0,3,2,1:T(8,128)S(1)} copy(f32[8,2,2,256,512]{4,3,2,1,0:T(8,128)} %all-to-all-done.1) | data formatting | bytes 33554432 | tf_op jit(solution)/shard_map/all_to_all | solution.py:116
  897.4 21.5 %fusion = (f32[2,8,256,512]{3,1,2,0:T(8,128)}, f32[2,8,256,512]{3,1,2,0:T(8,128)}) fusion(f32[8,256]{0,1:T(8,128)S(1)} %copy.152, f32[8,256]{0,1:T(8,128)S(1)} %copy.151, f32[2,256,512,8]{2,3,1,0:T(8,128)} %fusion.2, f32[2,256,512,8]{2,3,1,0:T(8,128)} %fusion.3, f32[2,256,512,8]{2,3,1,0:T(8,128)} %fusion.5, f32[2,2,8,256,512]{4,2,3,1,0:T(8,128)} %bitcast.294), kind=kOutput, calls=%fused_computation.25 | convolution fusion | flops 218104704 | bytes 50348032 | tf_op jit(solution)/shard_map/ka,fabm->fkbm/dot_general | solution.py:9
  918.9 26.4 %fusion.8 = f32[2,8,512,512]{2,3,1,0:T(8,128)} fusion(f32[2,8,256,512]{3,1,2,0:T(8,128)} %get-tuple-element.15, s32[256]{0:T(256)S(1)} %iota_add_fusion), kind=kOutput, calls=%fused_computation.35 | convolution fusion | flops 12886736896 | bytes 25166848 | tf_op jit(solution)/shard_map/qb,fkbm->fqkm/dot_general | solution.py:9
  945.2 25.8 %fusion.6 = f32[2,8,512,512]{2,3,1,0:T(8,128)S(1)} fusion(f32[2,8,256,512]{3,1,2,0:T(8,128)} %get-tuple-element.15, s32[256]{0:T(256)S(1)} %iota_add_fusion), kind=kOutput, calls=%fused_computation.33 | convolution fusion | flops 12886736896 | bytes 25166848 | tf_op jit(solution)/shard_map/qb,fkbm->fqkm/dot_general | solution.py:9
  971.1 49.7 %add_bitcast_fusion = f32[2,512,8,512]{3,1,2,0:T(8,128)} fusion(f32[2,8,512,512]{2,3,1,0:T(8,128)} %fusion.8, f32[2,8,256,512]{3,1,2,0:T(8,128)} %get-tuple-element.14, s32[256]{0:T(256)S(1)} %iota_add_fusion), kind=kOutput, calls=%fused_computation.15 | convolution fusion | flops 12890931200 | bytes 41944064 | tf_op jit(solution)/shard_map/qb,fkbm->fqkm/dot_general | solution.py:9
  1020.8 17.7 %copy.257 = f32[2,512,8,512]{3,2,1,0:T(8,128)} copy(f32[2,512,8,512]{3,1,2,0:T(8,128)} %add_bitcast_fusion) | data formatting | bytes 33554432 | tf_op jit(solution)/shard_map/add | solution.py:66
  1038.5 27.7 %subtract_bitcast_fusion = f32[2,512,8,512]{3,1,2,0:T(8,128)} fusion(f32[2,8,512,512]{2,3,1,0:T(8,128)S(1)} %fusion.6, f32[2,8,256,512]{3,1,2,0:T(8,128)} %get-tuple-element.14, s32[256]{0:T(256)S(1)} %iota_add_fusion), kind=kOutput, calls=%fused_computation.14 | convolution fusion | flops 12890931200 | bytes 41944064 | tf_op jit(solution)/shard_map/qb,fkbm->fqkm/dot_general | solution.py:9
  1066.3 19.3 %copy.256 = f32[2,512,8,512]{3,2,1,0:T(8,128)} copy(f32[2,512,8,512]{3,1,2,0:T(8,128)} %subtract_bitcast_fusion) | data formatting | bytes 33554432 | tf_op jit(solution)/shard_map/sub | solution.py:69
  1085.6 27.6 %multiply_reduce_fusion.3 = (f32[2,512,2]{1,0,2:T(2,128)S(1)}, f32[2,512,2]{1,0,2:T(2,128)S(1)}, f32[2,512,2]{1,0,2:T(2,128)S(1)}, f32[2,512,2]{1,0,2:T(2,128)S(1)}) fusion(f32[2,512,4096]{1,2,0:T(8,128)} %copy.204, f32[1,2,4096,512]{3,2,1,0:T(8,128)} %bitcast.297, f32[1,2,4096,512]{3,2,1,0:T(8,128)S(1)} %bitcast.296, f32[2,512,4096]{1,2,0:T(8,128)} %copy.205, ...), kind=kLoop, calls=%fused_computation.5 | loop fusion | flops 75489280 | bytes 100696064 | tf_op jit(solution)/shard_map/fk,ks,xfks->fxs/dot_general | solution.py:85
  (137 shorter events, 286.3 us)
Async XLA Ops:
  104.0 8.7 copy-start.10
  124.7 10.2 copy-start.8
  124.7 10.2 copy-start.14
  146.8 8.6 copy-start.9
  165.9 60.5 %copy-start.6 = (f32[256,8,512]{2,1,0:T(8,128)}, f32[256,8,512]{2,1,0:T(8,128)S(1)}, u32[]{:S(2)}) copy-start(f32[256,8,512]{2,1,0:T(8,128)S(1)} %get-tuple-element.25) | copy-start | bytes 12582916
  194.6 31.8 %copy-start.19 = (s32[4096]{0:T(1024)S(1)}, s32[4096]{0:T(1024)}, u32[]{:S(2)}) copy-start(s32[4096]{0:T(1024)} %param.10) | copy-start | bytes 49156
  247.8 9.5 copy-start.4
  247.8 9.5 copy-start.13
  278.6 9.5 copy-start.7
  278.6 9.5 copy-start.12
  309.6 9.5 copy-start.5
  309.6 9.5 copy-start.11
  340.4 7.9 copy-start.15
  340.4 7.9 copy-start.16
  348.3 7.7 copy-start.17
  482.9 370.7 %all-to-all-start.1 = ((f32[8,2,2,256,512]{4,3,2,1,0:T(8,128)}), f32[8,2,2,256,512]{4,3,2,1,0:T(8,128)}, u32[]{:S(2)}, u32[]{:S(2)}) async-start(f32[8,2,2,256,512]{4,3,2,1,0:T(8,128)} %copy.149), calls=%async_computation.1 | async-start | bytes 33554432 | tf_op jit(solution)/shard_map/all_to_all | solution.py:116
  490.2 40.1 %all-gather.2.cloned.1.call-start = ((), (), s32[]{:S(2)}) async-start(), calls=%async_computation.3 | async-start | bytes 25165824 | tf_op jit(solution)/shard_map/all_gather | solution.py:130
  498.6 0.8 copy-start.20
  498.6 2.6 copy-start.21
  498.6 14.1 %copy-start.27 = (f32[4]{0:T(128)S(1)}, f32[4]{0:T(128)}, u32[]{:S(2)}) copy-start(f32[4]{0:T(128)} %param.11) | copy-start | bytes 52
  498.6 626.3 %reduce-scatter.4.cloned.1.call-start = ((), (), s32[]{:S(2)}) async-start(), calls=%async_computation.4 | async-start | bytes 393216
  566.2 16.5 %copy-start.1 = (f32[2,512,4096]{1,0,2:T(2,128)S(1)}, f32[2,512,4096]{1,0,2:T(2,128)}, u32[]{:S(2)}) copy-start(f32[2,512,4096]{1,0,2:T(2,128)} %get-tuple-element.47) | copy-start | bytes 50331652
  582.7 8.9 copy-start.18
  611.7 16.5 %copy-start.2 = (f32[2,512,4096]{1,0,2:T(2,128)S(1)}, f32[2,512,4096]{1,0,2:T(2,128)}, u32[]{:S(2)}) copy-start(f32[2,512,4096]{1,0,2:T(2,128)} %get-tuple-element.49) | copy-start | bytes 50331652
  869.0 18.7 %copy-start = (f32[8,2,2,256,512]{4,0,3,2,1:T(8,128)}, f32[8,2,2,256,512]{4,0,3,2,1:T(8,128)S(1)}, u32[]{:S(2)}) copy-start(f32[8,2,2,256,512]{4,0,3,2,1:T(8,128)S(1)} %copy.258) | copy-start | bytes 50331652
  1066.3 19.4 %copy-start.3 = (f32[2,512,8,512]{3,2,1,0:T(8,128)S(1)}, f32[2,512,8,512]{3,2,1,0:T(8,128)}, u32[]{:S(2)}) copy-start(f32[2,512,8,512]{3,2,1,0:T(8,128)} %copy.257) | copy-start | bytes 50331652
  1113.2 18.7 %copy-start.22 = (s32[4]{0:T(128)S(1)}, s32[4]{0:T(128)}, u32[]{:S(2)}) copy-start(s32[4]{0:T(128)} %param.9) | copy-start | bytes 52
  1113.2 18.7 %copy-start.23 = (f32[256]{0:T(256)S(1)}, f32[256]{0:T(256)}, u32[]{:S(2)}) copy-start(f32[256]{0:T(256)} %get-tuple-element.12) | copy-start | bytes 3076
  1113.2 18.7 %copy-start.24 = (f32[256]{0:T(256)S(1)}, f32[256]{0:T(256)}, u32[]{:S(2)}) copy-start(f32[256]{0:T(256)} %compare_select_fusion.7) | copy-start | bytes 3076
  1113.2 18.7 %copy-start.25 = (f32[4]{0:T(128)S(1)}, f32[4]{0:T(128)}, u32[]{:S(2)}) copy-start(f32[4]{0:T(128)} %get-tuple-element.41) | copy-start | bytes 52
  1113.3 18.7 %copy-start.26 = (f32[4]{0:T(128)S(1)}, f32[4]{0:T(128)}, u32[]{:S(2)}) copy-start(f32[4]{0:T(128)} %get-tuple-element.42) | copy-start | bytes 52
Sparse Core Ops, SparseCore 0:
  498.8 31.4 all-gather.1
  1118.2 6.7 reduce-scatter.3
